TPU v7x, 8 devices: a whole 2x2x1 slice. The times are simulated.
8 devices in a mesh: dp: 2 (over y, z), tp: 4 (over x, core).
Axes of the slice: x: 2, y: 2, z: 1, core: 2. Of those that a mesh axis runs over, the one named last changes fastest.
Arguments:
- x: bfloat16 [256, 2048], P('dp'), parts along dimension 0
- w_gate: bfloat16 [2048, 6144], P(None, 'tp')
- w_up: bfloat16 [2048, 6144], P(None, 'tp')
- w_down: bfloat16 [6144, 2048], P('tp')
Outputs:
- output: bfloat16 [256, 2048], P('dp'), parts along dimension 0
There are 2 independent parts. A program takes and returns all parts, laid end to end along the dimension named above; an argument that names none is the same for every part.
All inputs are finite; a program needn't handle non-finite values.
Results may differ from a plain program's by a relative error of at most 0.016.
Values are sent between devices in bfloat16 or wider.
A program may use at most 2 GiB of HBM per device.

v0:
```python
import jax
import jax.numpy as jnp
from jax import lax
from jax.sharding import PartitionSpec as P


def solution(mesh):
    def step(x, w_gate, w_up, w_down):
        gate = jnp.dot(x, w_gate, preferred_element_type=jnp.float32)
        up = jnp.dot(x, w_up, preferred_element_type=jnp.float32)
        hidden = (jax.nn.silu(gate) * up).astype(jnp.bfloat16)
        term = jnp.dot(hidden, w_down, preferred_element_type=jnp.float32).astype(jnp.bfloat16)
        return lax.psum(term, "tp")

    return jax.shard_map(
        step,
        mesh=mesh,
        in_specs=(P("dp", None), P(None, "tp"), P(None, "tp"), P("tp", None)),
        out_specs=P("dp", None),
        check_vma=False,
    )
```

profile of v0, /device:TPU:0, one launch (start us, length us, event | category | flops | bytes accessed | tf_op | source)
XLA Modules:
  0.0 58.2 jit_solution(2721495395800748846)
XLA Ops:
  6.5 0.0 copy-start
  6.5 0.0 all-reduce.2.cloned.1.call-start
  6.5 1.0 %copy-done = bf16[128,2048]{1,0:T(8,128)(2,1)S(1)} copy-done((bf16[128,2048]{1,0:T(8,128)(2,1)S(1)}, bf16[128,2048]{1,0:T(8,128)(2,1)}, u32[]{:S(2)}) %copy-start) | copy-done | bytes 524312
  7.6 3.8 %fusion.3 = f32[128,1536]{1,0:T(8,128)S(1)} fusion(bf16[128,2048]{1,0:T(8,128)(2,1)S(1)} %copy-done, bf16[2048,1536]{1,0:T(8,128)(2,1)} %param.5), kind=kOutput, calls=%fused_computation.5 | convolution fusion | flops 805306368 | bytes 7602176 | tf_op jit(solution)/shard_map/dot_general | solution.py:9
  11.4 7.4 %convolution_convert_fusion = bf16[128,2048]{1,0:T(8,128)(2,1)} fusion(bf16[1536,2048]{1,0:T(8,128)(2,1)} %param.7, bf16[128,2048]{1,0:T(8,128)(2,1)S(1)} %copy-done, bf16[2048,1536]{1,0:T(8,128)(2,1)} %param.6, f32[128,1536]{1,0:T(8,128)S(1)} %fusion.3), kind=kOutput, calls=%fused_computation.2 | convolution fusion | flops 1612054528 | bytes 14417920 | tf_op jit(solution)/shard_map/dot_general | solution.py:12
  18.8 0.0 all-reduce.2.cloned.1.call-update
  18.8 30.7 %all-reduce.2.cloned.1.call-done = bf16[128,2048]{1,0:T(8,128)(2,1)} async-done(((bf16[128,2048]{1,0:T(8,128)(2,1)}), bf16[128,2048]{1,0:T(8,128)(2,1)}) %all-reduce.2.cloned.1.call-update) | async-done | bytes 524304 | tf_op jit(solution)/shard_map/psum | solution.py:13
  49.5 1.9 %copy.6 = bf16[128,2048]{1,0:T(8,128)(2,1)} copy(bf16[128,2048]{1,0:T(8,128)(2,1)} %all-reduce.2.cloned.1.call-done) | data formatting | bytes 1048576
Async XLA Ops:
  6.5 1.0 %copy-start = (bf16[128,2048]{1,0:T(8,128)(2,1)S(1)}, bf16[128,2048]{1,0:T(8,128)(2,1)}, u32[]{:S(2)}) copy-start(bf16[128,2048]{1,0:T(8,128)(2,1)} %param.4) | copy-start | bytes 1572868
  6.5 43.0 %all-reduce.2.cloned.1.call-start = ((), (), s32[]{:S(2)}) async-start(), calls=%async_computation | async-start | bytes 1048576 | tf_op jit(solution)/shard_map/psum | solution.py:13
Sparse Core Ops, SparseCore 0:
  18.9 30.5 all-reduce.1
where the time goes:
time: 58.5 us; the launch traced here: 58.2 us
  waiting for transfers between devices  30.7 us (52%)
  between operations  13.4 us (23%)
  matrix products  11.2 us (19%)
  local copies, waits for them, and re-layouts  2.92 us (5%)
    psum x1, waiting for transfers between devices, step(): return lax.psum(term, 'tp')  30.7 us
    dot_general x1, matrix products, step(): jnp.dot(hidden, w_down, preferred_element_type=jnp.float32)  7.42 us
    dot_general x1, matrix products, step(): gate = jnp.dot(x, w_gate, preferred_element_type=jnp.float32)  3.77 us
    unnamed x3, local copies, waits for them, and re-layouts  2.92 us
  transfers between devices with their start and end apart: 1, of which 1 were waited for; matrix products, arithmetic and copies ran while one was open for 0% of the time, Pallas kernels for 0%

commit v1 on v0

v1 whole, which is shorter than its diff:
```python
import jax
import jax.numpy as jnp
from jax import lax
from jax.experimental import pallas as pl
from jax.experimental.pallas import tpu as pltpu
from jax.sharding import PartitionSpec as P

ROWS = 128
D = 2048
F = 1536
FC = 256
NF = F // FC
HALF = D // 2
C = 256
NC = HALF // C


def kernel(
    x_hbm, wg_hbm, wu_hbm, wd_hbm, out,
    xv, wgv, wuv, wdv, h, tsend, trecv, own, ssend, srecv,
    x_sem, g_sem, u_sem, d_sem,
    ts_sem, tr_sem, ss_sem, sr_sem, ys_sem, yr_sem, yl_sem,
):
    me = lax.axis_index("tp")
    core = lax.rem(me, 2)
    sib = me + 1 - 2 * core
    opp = lax.rem(me + 2, 4)
    own_base = core * HALF
    sib_base = (1 - core) * HALF

    barrier = pltpu.get_barrier_semaphore()
    for other in (sib, opp):
        pl.semaphore_signal(barrier, inc=1, device_id={"tp": other}, device_id_type=pl.DeviceIdType.MESH)

    x_copy = pltpu.make_async_copy(x_hbm, xv, x_sem)
    x_copy.start()
    g_copies, u_copies, d_copies = [], [], []
    for j in range(NF):
        cols = pl.ds(j * FC, FC)
        g = pltpu.make_async_copy(wg_hbm.at[:, cols], wgv.at[j], g_sem.at[j])
        u = pltpu.make_async_copy(wu_hbm.at[:, cols], wuv.at[j], u_sem.at[j])
        g.start()
        u.start()
        g_copies.append(g)
        u_copies.append(u)
    for j in range(NC):
        for role, base in ((0, sib_base), (1, own_base)):
            cols = pl.ds(pl.multiple_of(base + j * C, C), C)
            d = pltpu.make_async_copy(wd_hbm.at[:, cols], wdv.at[2 * j + role], d_sem.at[2 * j + role])
            d.start()
            d_copies.append(d)

    x_copy.wait()
    for j in range(NF):
        g_copies[j].wait()
        gate = jnp.dot(xv[...], wgv[j], preferred_element_type=jnp.float32)
        u_copies[j].wait()
        up = jnp.dot(xv[...], wuv[j], preferred_element_type=jnp.float32)
        h[:, j * FC : (j + 1) * FC] = (jax.nn.silu(gate) * up).astype(jnp.bfloat16)

    pl.semaphore_wait(barrier, 2)

    def remote(src, dst, s, r, to):
        return pltpu.make_async_remote_copy(
            src_ref=src, dst_ref=dst, send_sem=s, recv_sem=r,
            device_id={"tp": to}, device_id_type=pl.DeviceIdType.MESH,
        )

    t_copies = [remote(tsend.at[j], trecv.at[j], ts_sem.at[j], tr_sem.at[j], sib) for j in range(NC)]
    s_copies = [remote(ssend.at[j], srecv.at[j], ss_sem.at[j], sr_sem.at[j], opp) for j in range(NC)]
    ysrc = ssend

    def down(j):
        d_copies[2 * j].wait()
        t = jnp.dot(h[...], wdv[2 * j], preferred_element_type=jnp.float32)
        tsend[j] = t.astype(jnp.bfloat16)
        t_copies[j].start()
        d_copies[2 * j + 1].wait()
        own[j] = jnp.dot(h[...], wdv[2 * j + 1], preferred_element_type=jnp.float32)

    def chip_sum(j):
        t_copies[j].wait_recv()
        ssend[j] = (own[j] + trecv[j].astype(jnp.float32)).astype(jnp.bfloat16)
        s_copies[j].start()

    for j in range(NC):
        down(j)
        if j >= 1:
            chip_sum(j - 1)
    chip_sum(NC - 1)

    y_copies = []
    for j in range(NC):
        s_copies[j].wait_recv()
        trecv[j] = (ssend[j].astype(jnp.float32) + srecv[j].astype(jnp.float32)).astype(jnp.bfloat16)
        cols = pl.ds(pl.multiple_of(own_base + j * C, C), C)
        yr = remote(trecv.at[j], out.at[:, cols], ys_sem.at[j], yr_sem.at[j], sib)
        yl = pltpu.make_async_copy(trecv.at[j], out.at[:, cols], yl_sem.at[j])
        yr.start()
        yl.start()
        y_copies.append((yr, yl))
    for j in range(NC):
        t_copies[j].wait_send()
        s_copies[j].wait_send()
        y_copies[j][1].wait()
        y_copies[j][0].wait()


def solution(mesh):
    bf, f32 = jnp.bfloat16, jnp.float32
    dma = pltpu.SemaphoreType.DMA

    def step(x, w_gate, w_up, w_down):
        hbm = lambda a: pltpu.with_memory_space_constraint(a, pltpu.HBM)
        return pl.pallas_call(
            kernel,
            out_shape=jax.ShapeDtypeStruct((ROWS, D), bf),
            in_specs=[pl.BlockSpec(memory_space=pl.ANY)] * 4,
            out_specs=pl.BlockSpec(memory_space=pl.ANY),
            scratch_shapes=[
                pltpu.VMEM((ROWS, D), bf),
                pltpu.VMEM((NF, D, FC), bf),
                pltpu.VMEM((NF, D, FC), bf),
                pltpu.VMEM((2 * NC, F, C), bf),
                pltpu.VMEM((ROWS, F), bf),
                pltpu.VMEM((NC, ROWS, C), bf),
                pltpu.VMEM((NC, ROWS, C), bf),
                pltpu.VMEM((NC, ROWS, C), f32),
                pltpu.VMEM((NC, ROWS, C), bf),
                pltpu.VMEM((NC, ROWS, C), bf),
                dma,
                dma((NF,)),
                dma((NF,)),
                dma((2 * NC,)),
                *[dma((NC,))] * 7,
            ],
            compiler_params=pltpu.CompilerParams(
                collective_id=0, has_side_effects=True, vmem_limit_bytes=60 * 2**20
            ),
        )(hbm(x), hbm(w_gate), hbm(w_up), hbm(w_down))

    return jax.shard_map(
        step,
        mesh=mesh,
        in_specs=(P("dp", None), P(None, "tp"), P(None, "tp"), P("tp", None)),
        out_specs=P("dp", None),
        check_vma=False,
    )
```

time: 58.5 us -> 25.8 us (0.44)
  waiting for transfers between devices: 30.7 us -> 0 us
  Pallas kernels: 0 us -> 23.8 us
  between operations: 13.4 us -> 0.01 us
  matrix products: 11.2 us -> 0 us
  local copies, waits for them, and re-layouts: 2.92 us -> 1.88 us
    psum x1 -> x0, waiting for transfers between devices: 30.7 us -> none  [step(): return lax.psum(term, 'tp')]
    pallas_call x0 -> x1, Pallas kernels: none -> 23.8 us  [step(): pl.pallas_call(kernel, out_shape=jax.ShapeDtypeStruct((ROWS, D), bf), in_...]
    dot_general x2 -> x0, matrix products: 11.2 us -> none  [the longest x1 7.42 us: step(): jnp.dot(hidden, w_down, preferred_element_type=jnp.float32)]
    unnamed x3 -> x1, local copies, waits for them, and re-layouts: 2.92 us -> 1.88 us
  transfers between devices with their start and end apart: 1 -> 0, of which waited for: 1 -> 0; matrix products, arithmetic and copies ran while one was open for 0% -> 0% of each run, Pallas kernels for 0% -> 0%
where the time goes in v1:
time: 25.8 us; the launch traced here: 25.6 us
  Pallas kernels  23.8 us (92%)
  local copies, waits for them, and re-layouts  1.88 us (7%)
    pallas_call x1, Pallas kernels, step(): pl.pallas_call(kernel, out_shape=jax.ShapeDtypeStruct((ROWS, D), bf), in_...  23.8 us
    unnamed x1, local copies, waits for them, and re-layouts  1.88 us

profile of v1, /device:TPU:0, one launch (start us, length us, event | category | flops | bytes accessed | tf_op | source)
XLA Modules:
  0.0 25.6 jit_solution(2032148380255844763)
XLA Ops:
  0.0 23.8 %shard_map.46 = bf16[128,2048]{1,0:T(8,128)(2,1)} custom-call(bf16[128,2048]{1,0:T(8,128)(2,1)} %x_hbm.1, bf16[2048,1536]{1,0:T(8,128)(2,1)} %wg_hbm.1, bf16[2048,1536]{1,0:T(8,128)(2,1)} %wu_hbm.1, bf16[1536,2048]{1,0:T(8,128)(2,1)} %wd_hbm.1), custom_call_target="tpu_custom_call" | custom-call | tf_op jit(solution)/shard_map/pallas_call | solution.py:115
  23.8 1.9 %copy.6 = bf16[128,2048]{1,0:T(8,128)(2,1)} copy(bf16[128,2048]{1,0:T(8,128)(2,1)} %shard_map.46) | data formatting | bytes 1048576

commit v2 on v0

v2 whole, which is shorter than its diff:
```python
import jax
import jax.numpy as jnp
from jax import lax
from jax.experimental import pallas as pl
from jax.experimental.pallas import tpu as pltpu
from jax.sharding import PartitionSpec as P

ROWS = 128
D = 2048
F = 1536
HALF = D // 2
HIDDEN = (256, 256, 256, 256, 256, 256)
C = 128
NC = HALF // C
LAG = 3
MESH = pl.DeviceIdType.MESH
scope = jax.named_scope


def remote(src, dst, send, recv, to):
    return pltpu.make_async_remote_copy(
        src_ref=src, dst_ref=dst, send_sem=send, recv_sem=recv, device_id={"tp": to}, device_id_type=MESH
    )


def block(x_hbm, wg_hbm, wu_hbm, wd_hbm, out, xv, wgv, wuv, wdv, h, tsend, trecv, own, ssend, srecv,
          in_sem, ts_sem, tr_sem, ss_sem, sr_sem, ys_sem, yr_sem):
    me = lax.axis_index("tp")
    core = lax.rem(me, 2)
    sib = me + 1 - 2 * core
    opp = lax.rem(me + 2, 4)

    barrier = pltpu.get_barrier_semaphore()
    for other in (sib, opp):
        pl.semaphore_signal(barrier, inc=1, device_id={"tp": other}, device_id_type=MESH)

    copies = []

    def load(src, dst):
        copies.append(pltpu.make_async_copy(src, dst, in_sem.at[len(copies)]))
        copies[-1].start()
        return copies[-1]

    x_copy = load(x_hbm, xv)
    hidden, at = [], 0
    for width in HIDDEN:
        cols = slice(at, at + width)
        at += width
        src = pl.ds(cols.start, width)
        hidden.append((cols, load(wg_hbm.at[:, src], wgv.at[:, src]), load(wu_hbm.at[:, src], wuv.at[:, src])))
    down = []
    for j in range(NC):
        for role in range(2):
            base = (1 - core if role == 0 else core) * HALF
            src = pl.ds(pl.multiple_of(base + j * C, C), C)
            down.append(load(wd_hbm.at[:, src], wdv.at[2 * j + role]))

    with scope("wait_x"):
        x_copy.wait()
    for k, (cols, g_copy, u_copy) in enumerate(hidden):
        with scope(f"wait_g{k}"):
            g_copy.wait()
            u_copy.wait()
        with scope(f"hid{k}"):
            gate = jnp.dot(xv[...], wgv[:, cols], preferred_element_type=jnp.float32)
            up = jnp.dot(xv[...], wuv[:, cols], preferred_element_type=jnp.float32)
            h[:, cols] = (jax.nn.silu(gate) * up).astype(jnp.bfloat16)
    with scope("barrier"):
        pl.semaphore_wait(barrier, 2)

    t_copies = [remote(tsend.at[j], trecv.at[j], ts_sem.at[j], tr_sem.at[j], sib) for j in range(NC)]
    s_copies = [remote(ssend.at[j], srecv.at[j], ss_sem.at[j], sr_sem.at[j], opp) for j in range(NC)]

    def chip_sum(j):
        with scope(f"wait_t{j}"):
            t_copies[j].wait_recv()
        with scope(f"sum{j}"):
            ssend[j] = (own[j] + trecv[j].astype(jnp.float32)).astype(jnp.bfloat16)
            s_copies[j].start()

    for j in range(NC):
        with scope(f"wait_d{j}"):
            down[2 * j].wait()
            down[2 * j + 1].wait()
        with scope(f"down{j}"):
            tsend[j] = jnp.dot(h[...], wdv[2 * j], preferred_element_type=jnp.float32).astype(jnp.bfloat16)
            t_copies[j].start()
            own[j] = jnp.dot(h[...], wdv[2 * j + 1], preferred_element_type=jnp.float32)
        if j >= LAG:
            chip_sum(j - LAG)
    for j in range(NC - LAG, NC):
        chip_sum(j)

    y_copies = []
    for j in range(NC):
        with scope(f"wait_s{j}"):
            s_copies[j].wait_recv()
        with scope(f"fin{j}"):
            out[core, j] = (ssend[j].astype(jnp.float32) + srecv[j].astype(jnp.float32)).astype(jnp.bfloat16)
            y_copies.append(remote(out.at[core, j], out.at[core, j], ys_sem.at[j], yr_sem.at[j], sib))
            y_copies[-1].start()
    with scope("drain_s"):
        for j in range(NC):
            t_copies[j].wait_send()
            s_copies[j].wait_send()
    with scope("drain_y"):
        for j in range(NC):
            y_copies[j].wait()


def store(y_vmem, y_hbm, sem):
    copies = []
    for c in range(2):
        for j in range(NC):
            dst = y_hbm.at[:, pl.ds(c * HALF + j * C, C)]
            copies.append(pltpu.make_async_copy(y_vmem.at[c, j], dst, sem.at[c * NC + j]))
            copies[-1].start()
    for copy in copies:
        copy.wait()


def solution(mesh):
    bf, f32 = jnp.bfloat16, jnp.float32
    dma = pltpu.SemaphoreType.DMA
    anywhere = pl.BlockSpec(memory_space=pl.ANY)
    vmem = pl.BlockSpec(memory_space=pltpu.VMEM)

    def step(x, w_gate, w_up, w_down):
        hbm = lambda a: pltpu.with_memory_space_constraint(a, pltpu.HBM)
        chunks = lambda dtype: pltpu.VMEM((NC, ROWS, C), dtype)
        y = pl.pallas_call(
            block,
            out_shape=pltpu.VMEM((2, NC, ROWS, C), bf),
            in_specs=[anywhere] * 4,
            out_specs=vmem,
            scratch_shapes=[
                pltpu.VMEM((ROWS, D), bf),
                pltpu.VMEM((D, F), bf),
                pltpu.VMEM((D, F), bf),
                pltpu.VMEM((2 * NC, F, C), bf),
                pltpu.VMEM((ROWS, F), bf),
                chunks(bf),
                chunks(bf),
                chunks(f32),
                chunks(bf),
                chunks(bf),
                dma((1 + 2 * len(HIDDEN) + 2 * NC,)),
                *[dma((NC,))] * 6,
            ],
            compiler_params=pltpu.CompilerParams(
                collective_id=0, has_side_effects=True, vmem_limit_bytes=50 * 2**20
            ),
            name="block",
        )(hbm(x), hbm(w_gate), hbm(w_up), hbm(w_down))
        return pl.pallas_call(
            store,
            out_shape=jax.ShapeDtypeStruct((ROWS, D), bf),
            in_specs=[vmem],
            out_specs=anywhere,
            scratch_shapes=[dma((2 * NC,))],
            name="store",
        )(pltpu.with_memory_space_constraint(y, pltpu.VMEM))

    return jax.shard_map(
        step,
        mesh=mesh,
        in_specs=(P("dp", None), P(None, "tp"), P(None, "tp"), P("tp", None)),
        out_specs=P("dp", None),
        check_vma=False,
    )
```

time: 58.5 us -> 19.8 us (0.34)
  waiting for transfers between devices: 30.7 us -> 0 us
  Pallas kernels: 0 us -> 19.7 us
  between operations: 13.4 us -> 0.01 us
  matrix products: 11.2 us -> 0 us
  local copies, waits for them, and re-layouts: 2.92 us -> 0 us
    psum x1 -> x0, waiting for transfers between devices: 30.7 us -> none  [step(): return lax.psum(term, 'tp')]
    pallas_call x0 -> x2, Pallas kernels: none -> 19.7 us  [the longest x1 18.8 us: step(): pl.pallas_call(block, out_shape=pltpu.VMEM((2, NC, ROWS, C), bf), in_spec...]
    dot_general x2 -> x0, matrix products: 11.2 us -> none  [the longest x1 7.42 us: step(): jnp.dot(hidden, w_down, preferred_element_type=jnp.float32)]
    unnamed x3 -> x0, local copies, waits for them, and re-layouts: 2.92 us -> none
  transfers between devices with their start and end apart: 1 -> 0, of which waited for: 1 -> 0; matrix products, arithmetic and copies ran while one was open for 0% -> 0% of each run, Pallas kernels for 0% -> 0%
where the time goes in v2:
time: 19.8 us; the launch traced here: 19.7 us
  Pallas kernels  19.7 us (99%)
    pallas_call x1, Pallas kernels, step(): pl.pallas_call(block, out_shape=pltpu.VMEM((2, NC, ROWS, C), bf), in_spec...  18.8 us
    pallas_call x1, Pallas kernels, step(): pl.pallas_call(store, out_shape=jax.ShapeDtypeStruct((ROWS, D), bf), in_s...  0.92 us

profile of v2, /device:TPU:0, one launch (start us, length us, event | category | flops | bytes accessed | tf_op | source)
XLA Modules:
  0.0 19.7 jit_solution(8871693437607027218)
XLA Ops:
  0.0 18.8 %block.1.y_vmem = bf16[2,8,128,128]{3,2,1,0:T(8,128)(2,1)S(1)} custom-call(bf16[128,2048]{1,0:T(8,128)(2,1)} %x_hbm.1, bf16[2048,1536]{1,0:T(8,128)(2,1)} %wg_hbm.1, bf16[2048,1536]{1,0:T(8,128)(2,1)} %wu_hbm.1, bf16[1536,2048]{1,0:T(8,128)(2,1)} %wd_hbm.1), custom_call_target="tpu_custom_call" | custom-call | tf_op jit(solution)/shard_map/block/pallas_call | solution.py:131
  18.8 0.9 %store.1 = bf16[128,2048]{1,0:T(8,128)(2,1)} custom-call(bf16[2,8,128,128]{3,2,1,0:T(8,128)(2,1)S(1)} %block.1.y_vmem), custom_call_target="tpu_custom_call" | custom-call | tf_op jit(solution)/shard_map/store/pallas_call | solution.py:155

commit v3 on v0

v3 whole, which is shorter than its diff:
```python
import jax
import jax.numpy as jnp
from jax import lax
from jax.experimental import pallas as pl
from jax.experimental.pallas import tpu as pltpu
from jax.sharding import PartitionSpec as P

ROWS = 128
D = 2048
F = 1536
HIDDEN = (512, 512, 256, 256)
DOWN = (256, 256, 512, 1024)
C = 128
N = D // C
B = 2 * C
LAG = (1, 3)

OWNER = (0, 1, 0, 1, 0, 1, 0, 1, 0, 1, 0, 1, 1, 1, 1, 1)
DIRECT = (1,)
SHARED = (15,)
MESH = pl.DeviceIdType.MESH
scope = jax.named_scope


def columns(k):
    return pl.ds(k * C, C)


def block(x_hbm, wg_hbm, wu_hbm, wd_hbm, out, xv, wgv, wuv, wdv, h, own, tsend, trecv, ssend, srecv, drecv,
          in_sem, t_sem, s_sem, d_sem, y_sem, b_sem, send_sem):
    me = lax.axis_index("tp")
    core = lax.rem(me, 2)
    sib = me + 1 - 2 * core
    opp = lax.rem(me + 2, 4)
    cross = 3 - me
    f32 = jnp.float32

    barrier = pltpu.get_barrier_semaphore()
    for other in (sib, opp, cross):
        pl.semaphore_signal(barrier, inc=1, device_id={"tp": other}, device_id_type=MESH)

    copies = []

    def load(src, dst):
        copies.append(pltpu.make_async_copy(src, dst, in_sem.at[len(copies)]))
        copies[-1].start()
        return copies[-1]

    x_copy = load(x_hbm, xv)
    hidden, at = [], 0
    for width in HIDDEN:
        src = pl.ds(at, width)
        hidden.append((slice(at, at + width), load(wg_hbm.at[:, src], wgv.at[:, src]), load(wu_hbm.at[:, src], wuv.at[:, src])))
        at += width
    down, at = {}, 0
    for width in DOWN:
        src = pl.ds(at, width)
        down[at] = load(wd_hbm.at[:, src], wdv.at[:, src])
        at += width

    with scope("wait_x"):
        x_copy.wait()
    for k, (cols, g_copy, u_copy) in enumerate(hidden):
        with scope(f"wait_g{k}"):
            g_copy.wait()
            u_copy.wait()
        with scope(f"hid{k}"):
            gate = jnp.dot(xv[...], wgv[:, cols], preferred_element_type=f32)
            up = jnp.dot(xv[...], wuv[:, cols], preferred_element_type=f32)
            h[:, cols] = (jax.nn.silu(gate) * up).astype(jnp.bfloat16)
    with scope("barrier"):
        pl.semaphore_wait(barrier, 3)

    def remote(src, dst, recv, to):
        return pltpu.make_async_remote_copy(
            src_ref=src, dst_ref=dst, send_sem=send_sem, recv_sem=recv, device_id={"tp": to}, device_id_type=MESH
        )

    slot = [OWNER[:k].count(OWNER[k]) for k in range(N)]
    t_copy = lambda k: remote(tsend.at[k], trecv.at[k], t_sem.at[slot[k]], sib)
    s_copy = lambda k, to: remote(ssend.at[k], srecv.at[k], s_sem.at[slot[k]], to)
    b_copy = lambda k: remote(ssend.at[k], ssend.at[k], b_sem.at[SHARED.index(k)], sib)
    y_copy = lambda k: remote(out.at[:, columns(k)], out.at[:, columns(k)], y_sem, sib)
    direct = [k for k in range(N) if k in DIRECT]
    shared = [k for k in range(N) if k in SHARED]
    sent = {0: 0, 1: 0}

    def term(j):
        if j * B in down:
            with scope(f"wait_d{j}"):
                down[j * B].wait()
        with scope(f"down{j}"):
            value = jnp.dot(h[...], wdv[:, j * B : (j + 1) * B], preferred_element_type=f32)
            for i in range(B // C):
                k = j * (B // C) + i
                part = value[:, i * C : (i + 1) * C]
                own[k] = part
                tsend[k] = part.astype(jnp.bfloat16)
            for i in range(B // C):
                k = j * (B // C) + i
                if k in DIRECT:
                    i = direct.index(k)
                    for c in range(2):
                        to = opp if c == OWNER[k] else cross
                        sent[c] += 1

                        @pl.when(core == c)
                        def _(to=to, i=i, c=c, k=k):
                            remote(tsend.at[k], drecv.at[2 * i + c], d_sem.at[2 * i + c], to).start()

                sent[1 - OWNER[k]] += 1

                @pl.when(core != OWNER[k])
                def _(k=k):
                    t_copy(k).start()

    def chip_sum(j, c):
        chunks = [k for k in range(j * (B // C), (j + 1) * (B // C)) if OWNER[k] == c and k not in DIRECT]
        sent[c] += len(chunks) + 2 * len([k for k in chunks if k in SHARED])

        @pl.when(core == c)
        def _():
            for k in chunks:
                with scope(f"wait_t{k}"):
                    t_copy(k).wait_recv()
                with scope(f"sum{k}"):
                    ssend[k] = (own[k] + trecv[k].astype(f32)).astype(jnp.bfloat16)
                    if k in SHARED:
                        s_copy(k, cross).start()
                    s_copy(k, opp).start()
                    if k in SHARED:
                        b_copy(k).start()

    steps = D // B
    for j in range(steps + max(LAG)):
        if j < steps:
            term(j)
        for c in range(2):
            if 0 <= j - LAG[c] < steps:
                chip_sum(j - LAG[c], c)

    for c in range(2):
        mine = [k for k in range(N) if OWNER[k] == c and k not in SHARED]
        theirs = [k for k in range(N) if OWNER[k] != c and k not in SHARED]
        sent[c] += len(mine)

        @pl.when(core == c)
        def _(c=c, mine=mine, theirs=theirs):
            for k in mine:
                if k in DIRECT:
                    i = direct.index(k)
                    with scope(f"wait_s{k}"):
                        t_copy(k).wait_recv()
                        for p in range(2):
                            remote(tsend.at[k], drecv.at[2 * i + p], d_sem.at[2 * i + p], opp).wait_recv()
                    here = tsend[k].astype(f32) + trecv[k].astype(f32)
                    there = drecv[2 * i + c].astype(f32) + drecv[2 * i + 1 - c].astype(f32)
                else:
                    with scope(f"wait_s{k}"):
                        s_copy(k, opp).wait_recv()
                    here, there = ssend[k].astype(f32), srecv[k].astype(f32)
                with scope(f"fin{k}"):
                    out[:, columns(k)] = (here + there).astype(jnp.bfloat16)
                    y_copy(k).start()
            for k in shared:
                with scope(f"wait_s{k}"):
                    s_copy(k, opp).wait_recv()
                    if OWNER[k] != c:
                        b_copy(k).wait_recv()
                with scope(f"fin{k}"):
                    out[:, columns(k)] = (ssend[k].astype(f32) + srecv[k].astype(f32)).astype(jnp.bfloat16)
            with scope("drain_send"):
                every = tsend.at[pl.ds(0, N)]
                total = sent[c]
                while total:
                    n = min(total, N)
                    remote(tsend.at[pl.ds(0, n)], trecv.at[pl.ds(0, n)], y_sem, sib).wait_send()
                    total -= n
            with scope("drain_y"):
                n = len(theirs)
                remote(tsend.at[pl.ds(0, n)], trecv.at[pl.ds(0, n)], y_sem, sib).wait_recv()


def store(y_vmem, y_hbm, sem):
    copy = pltpu.make_async_copy(y_vmem, y_hbm, sem)
    copy.start()
    copy.wait()


def solution(mesh):
    bf = jnp.bfloat16
    dma = pltpu.SemaphoreType.DMA
    anywhere = pl.BlockSpec(memory_space=pl.ANY)
    vmem = pl.BlockSpec(memory_space=pltpu.VMEM)

    def step(x, w_gate, w_up, w_down):
        hbm = lambda a: pltpu.with_memory_space_constraint(a, pltpu.HBM)
        chunks = lambda n, dtype: pltpu.VMEM((n, ROWS, C), dtype)
        y = pl.pallas_call(
            block,
            out_shape=pltpu.VMEM((ROWS, D), bf),
            in_specs=[anywhere] * 4,
            out_specs=vmem,
            scratch_shapes=[
                pltpu.VMEM((ROWS, D), bf),
                pltpu.VMEM((D, F), bf),
                pltpu.VMEM((D, F), bf),
                pltpu.VMEM((F, D), bf),
                pltpu.VMEM((ROWS, F), bf),
                chunks(N, jnp.float32),
                chunks(N, bf),
                chunks(N, bf),
                chunks(N, bf),
                chunks(N, bf),
                chunks(2 * max(1, len(DIRECT)), bf),
                dma((1 + 2 * len(HIDDEN) + len(DOWN),)),
                dma((max(OWNER.count(0), OWNER.count(1)),)),
                dma((max(OWNER.count(0), OWNER.count(1)),)),
                dma((2 * max(1, len(DIRECT)),)),
                dma,
                dma((max(1, len(SHARED)),)),
                dma,
            ],
            compiler_params=pltpu.CompilerParams(
                collective_id=0, has_side_effects=True, vmem_limit_bytes=50 * 2**20
            ),
            name="block",
        )(hbm(x), hbm(w_gate), hbm(w_up), hbm(w_down))
        return pl.pallas_call(
            store,
            out_shape=jax.ShapeDtypeStruct((ROWS, D), bf),
            in_specs=[vmem],
            out_specs=anywhere,
            scratch_shapes=[dma],
            name="store",
        )(pltpu.with_memory_space_constraint(y, pltpu.VMEM))

    return jax.shard_map(
        step,
        mesh=mesh,
        in_specs=(P("dp", None), P(None, "tp"), P(None, "tp"), P("tp", None)),
        out_specs=P("dp", None),
        check_vma=False,
    )
```

time: 58.5 us -> 17.8 us (0.30)
  waiting for transfers between devices: 30.7 us -> 0 us
  Pallas kernels: 0 us -> 17.7 us
  between operations: 13.4 us -> 0.01 us
  matrix products: 11.2 us -> 0 us
  local copies, waits for them, and re-layouts: 2.92 us -> 0 us
    psum x1 -> x0, waiting for transfers between devices: 30.7 us -> none  [step(): return lax.psum(term, 'tp')]
    pallas_call x0 -> x2, Pallas kernels: none -> 17.7 us  [the longest x1 16.9 us: step(): pl.pallas_call(block, out_shape=pltpu.VMEM((ROWS, D), bf), in_specs=[anyw...]
    dot_general x2 -> x0, matrix products: 11.2 us -> none  [the longest x1 7.42 us: step(): jnp.dot(hidden, w_down, preferred_element_type=jnp.float32)]
    unnamed x3 -> x0, local copies, waits for them, and re-layouts: 2.92 us -> none
  transfers between devices with their start and end apart: 1 -> 0, of which waited for: 1 -> 0; matrix products, arithmetic and copies ran while one was open for 0% -> 0% of each run, Pallas kernels for 0% -> 0%
where the time goes in v3:
time: 17.8 us; the launch traced here: 17.7 us
  Pallas kernels  17.7 us (99%)
    pallas_call x1, Pallas kernels, step(): pl.pallas_call(block, out_shape=pltpu.VMEM((ROWS, D), bf), in_specs=[anyw...  16.9 us
    pallas_call x1, Pallas kernels, step(): pl.pallas_call(store, out_shape=jax.ShapeDtypeStruct((ROWS, D), bf), in_s...  0.8 us

profile of v3, /device:TPU:0, one launch (start us, length us, event | category | flops | bytes accessed | tf_op | source)
XLA Modules:
  0.0 17.7 jit_solution(4295665316425793390)
XLA Ops:
  0.0 16.9 %block.1.y_vmem = bf16[128,2048]{1,0:T(8,128)(2,1)S(1)} custom-call(bf16[128,2048]{1,0:T(8,128)(2,1)} %x_hbm.1, bf16[2048,1536]{1,0:T(8,128)(2,1)} %wg_hbm.1, bf16[2048,1536]{1,0:T(8,128)(2,1)} %wu_hbm.1, bf16[1536,2048]{1,0:T(8,128)(2,1)} %wd_hbm.1), custom_call_target="tpu_custom_call" | custom-call | tf_op jit(solution)/shard_map/block/pallas_call | solution.py:199
  16.9 0.8 %store.1 = bf16[128,2048]{1,0:T(8,128)(2,1)} custom-call(bf16[128,2048]{1,0:T(8,128)(2,1)S(1)} %block.1.y_vmem), custom_call_target="tpu_custom_call" | custom-call | tf_op jit(solution)/shard_map/store/pallas_call | solution.py:229

commit v4 on v3

v4 whole, which is shorter than its diff:
```python
import jax
import jax.numpy as jnp
from jax import lax
from jax.experimental import pallas as pl
from jax.experimental.pallas import tpu as pltpu
from jax.sharding import PartitionSpec as P

ROWS = 128
D = 2048
F = 1536
HIDDEN = ((768, (1024, 1024)), (768, (1024, 512, 512)))
DOWN = (256, 256, 512, 1024)
C = 128
N = D // C
STEPS = ((0, 1), (2, 3), (4, 5, 6, 7), (8, 9, 10, 11), (12, 13, 14, 15))
LAG = (1, 2)

GROUPS = (((0, 2), (4, 6), (8,), (10,)), ((5, 7), (9, 11), (12, 13), (14,)))
DIRECT = (1, 3)
SHARED = (15,)
MESH = pl.DeviceIdType.MESH
scope = jax.named_scope
OWNER = {k: c for c in range(2) for group in GROUPS[c] for k in group} | {k: 1 for k in DIRECT + SHARED}


def columns(k):
    return pl.ds(k * C, C)


def block(x_hbm, wg_hbm, wu_hbm, wd_hbm, out, xv, guv, part, wdv, h, own, tsend, trecv, ssend, srecv, drecv,
          in_sem, t_sem, s_sem, d_sem, y_sem, b_sem, send_sem):
    me = lax.axis_index("tp")
    core = lax.rem(me, 2)
    sib = me + 1 - 2 * core
    opp = lax.rem(me + 2, 4)
    cross = 3 - me
    f32 = jnp.float32

    barrier = pltpu.get_barrier_semaphore()
    for other in (sib, opp, cross):
        pl.semaphore_signal(barrier, inc=1, device_id={"tp": other}, device_id_type=MESH)

    n_sem = 0

    def load(*pairs):
        nonlocal n_sem
        for src, dst in pairs:
            pltpu.make_async_copy(src, dst, in_sem.at[n_sem]).start()
        n_sem += 1
        return n_sem - 1

    def loaded(ref, n):
        pltpu.make_async_copy(ref, ref, in_sem.at[n]).wait()

    x_copy = load((x_hbm, xv))
    hidden, at = [], 0
    for width, depths in HIDDEN:
        cols, top, pieces = pl.ds(at, width), 0, []
        for depth in depths:
            rows = pl.ds(top, depth)
            n = load((wg_hbm.at[rows, cols], guv.at[0, rows, cols]), (wu_hbm.at[rows, cols], guv.at[1, rows, cols]))
            pieces.append((n, top, depth))
            top += depth
        hidden.append((at, width, pieces))
        at += width
    down, at = {}, 0
    for width in DOWN:
        cols = pl.ds(at, width)
        down[at // C] = (load((wd_hbm.at[:, cols], wdv.at[:, cols])), cols)
        at += width

    with scope("wait_x"):
        loaded(xv, x_copy)
    for c, (at, width, pieces) in enumerate(hidden):
        cols = slice(at, at + width)
        for n, top, depth in pieces:
            with scope(f"wait_g{c}_{top}"):
                loaded(guv.at[:, pl.ds(top, depth), pl.ds(at, width)], n)
            with scope(f"hid{c}_{top}"):
                rows = slice(top, top + depth)
                gate = jnp.dot(xv[:, rows], guv[0, rows, cols], preferred_element_type=f32)
                up = jnp.dot(xv[:, rows], guv[1, rows, cols], preferred_element_type=f32)
                if top > 0:
                    gate, up = gate + part[0, :, :width], up + part[1, :, :width]
                if top + depth < D:
                    part[0, :, :width], part[1, :, :width] = gate, up
                else:
                    h[:, cols] = (jax.nn.silu(gate) * up).astype(jnp.bfloat16)
    with scope("barrier"):
        pl.semaphore_wait(barrier, 3)

    def remote(src, dst, recv, to):
        return pltpu.make_async_remote_copy(
            src_ref=src, dst_ref=dst, send_sem=send_sem, recv_sem=recv, device_id={"tp": to}, device_id_type=MESH
        )

    def wait_recv(sem, n):
        remote(tsend.at[pl.ds(0, n)], trecv.at[pl.ds(0, n)], sem, sib).wait_recv()

    group_of = {k: g for c in range(2) for g, group in enumerate(GROUPS[c]) for k in group}
    shared_sem = s_sem.at[max(len(groups) for groups in GROUPS)]
    s_copy = lambda k, to: remote(ssend.at[k], srecv.at[k], shared_sem if k in SHARED else s_sem.at[group_of[k]], to)
    y_copy = lambda k: remote(out.at[:, columns(k)], out.at[:, columns(k)], y_sem, sib)
    sent = {0: 0, 1: 0}

    def term(j):
        chunks = STEPS[j]
        if chunks[0] in down:
            n, cols = down[chunks[0]]
            with scope(f"wait_d{j}"):
                loaded(wdv.at[:, cols], n)
        with scope(f"down{j}"):
            value = jnp.dot(h[...], wdv[:, chunks[0] * C : (chunks[-1] + 1) * C], preferred_element_type=f32)
            for i, k in enumerate(chunks):
                own[k] = value[:, i * C : (i + 1) * C]
                tsend[k] = value[:, i * C : (i + 1) * C].astype(jnp.bfloat16)
            for c in range(2):

                @pl.when(core == c)
                def _(c=c):
                    for k in chunks:
                        if k in DIRECT:
                            place = drecv.at[2 * DIRECT.index(k) + c]
                            remote(tsend.at[k], place, d_sem, opp if c == OWNER[k] else cross).start()
                            sent[c] += 1
                    for k in chunks:
                        if OWNER[k] != c:
                            remote(tsend.at[k], trecv.at[k], t_sem.at[j], sib).start()
                            sent[c] += 1

    def chip_sum(j, c):
        chunks = [k for k in STEPS[j] if OWNER[k] == c]

        @pl.when(core == c)
        def _():
            if any(k not in DIRECT for k in chunks):
                with scope(f"wait_t{j}"):
                    wait_recv(t_sem.at[j], len(chunks))
            for k in chunks:
                if k in DIRECT:
                    continue
                with scope(f"sum{k}"):
                    ssend[k] = (own[k] + trecv[k].astype(f32)).astype(jnp.bfloat16)
                    if k in SHARED:
                        s_copy(k, cross).start()
                    s_copy(k, opp).start()
                    if k in SHARED:
                        remote(ssend.at[k], ssend.at[k], b_sem, sib).start()
                    sent[c] += 3 if k in SHARED else 1

    for j in range(len(STEPS) + max(LAG)):
        if j < len(STEPS):
            term(j)
        for c in range(2):
            if 0 <= j - LAG[c] < len(STEPS):
                chip_sum(j - LAG[c], c)

    for c in range(2):

        @pl.when(core == c)
        def _(c=c):
            def finish(k, here, there):
                with scope(f"fin{k}"):
                    out[:, columns(k)] = (here + there).astype(jnp.bfloat16)
                    if k not in SHARED:
                        y_copy(k).start()
                        sent[c] += 1

            if c == 1 and DIRECT:
                with scope("wait_direct"):
                    wait_recv(d_sem, 2 * len(DIRECT))
                    for j, chunks in enumerate(STEPS):
                        mine = [k for k in chunks if OWNER[k] == 1]
                        if mine and all(k in DIRECT for k in mine):
                            wait_recv(t_sem.at[j], len(mine))
                for i, k in enumerate(DIRECT):
                    here = tsend[k].astype(f32) + trecv[k].astype(f32)
                    finish(k, here, drecv[2 * i + 1].astype(f32) + drecv[2 * i].astype(f32))
            for group in GROUPS[c]:
                with scope(f"wait_s{group[0]}"):
                    wait_recv(s_sem.at[group_of[group[0]]], len(group))
                for k in group:
                    finish(k, ssend[k].astype(f32), srecv[k].astype(f32))
            if SHARED:
                with scope("wait_shared"):
                    wait_recv(shared_sem, len(SHARED))
                    if c == 0:
                        wait_recv(b_sem, len(SHARED))
            for k in SHARED:
                finish(k, ssend[k].astype(f32), srecv[k].astype(f32))
            with scope("drain_send"):
                total = sent[c]
                while total:
                    n = min(total, N)
                    remote(tsend.at[pl.ds(0, n)], trecv.at[pl.ds(0, n)], y_sem, sib).wait_send()
                    total -= n
            with scope("drain_y"):
                wait_recv(y_sem, len([k for k in range(N) if OWNER[k] != c and k not in SHARED]))


def store(y_vmem, y_hbm, sem):
    copy = pltpu.make_async_copy(y_vmem, y_hbm, sem)
    copy.start()
    copy.wait()


def solution(mesh):
    bf = jnp.bfloat16
    dma = pltpu.SemaphoreType.DMA
    anywhere = pl.BlockSpec(memory_space=pl.ANY)
    vmem = pl.BlockSpec(memory_space=pltpu.VMEM)

    def step(x, w_gate, w_up, w_down):
        hbm = lambda a: pltpu.with_memory_space_constraint(a, pltpu.HBM)
        chunks = lambda n, dtype: pltpu.VMEM((n, ROWS, C), dtype)
        y = pl.pallas_call(
            block,
            out_shape=pltpu.VMEM((ROWS, D), bf),
            in_specs=[anywhere] * 4,
            out_specs=vmem,
            scratch_shapes=[
                pltpu.VMEM((ROWS, D), bf),
                pltpu.VMEM((2, D, F), bf),
                pltpu.VMEM((2, ROWS, max(width for width, _ in HIDDEN)), jnp.float32),
                pltpu.VMEM((F, D), bf),
                pltpu.VMEM((ROWS, F), bf),
                chunks(N, jnp.float32),
                chunks(N, bf),
                chunks(N, bf),
                chunks(N, bf),
                chunks(N, bf),
                chunks(2 * max(1, len(DIRECT)), bf),
                dma((1 + sum(len(depths) for _, depths in HIDDEN) + len(DOWN),)),
                dma((len(STEPS),)),
                dma((1 + max(len(groups) for groups in GROUPS),)),
                *[dma] * 4,
            ],
            compiler_params=pltpu.CompilerParams(
                collective_id=0, has_side_effects=True, vmem_limit_bytes=50 * 2**20
            ),
            name="block",
        )(hbm(x), hbm(w_gate), hbm(w_up), hbm(w_down))
        return pl.pallas_call(
            store,
            out_shape=jax.ShapeDtypeStruct((ROWS, D), bf),
            in_specs=[vmem],
            out_specs=anywhere,
            scratch_shapes=[dma],
            name="store",
        )(pltpu.with_memory_space_constraint(y, pltpu.VMEM))

    return jax.shard_map(
        step,
        mesh=mesh,
        in_specs=(P("dp", None), P(None, "tp"), P(None, "tp"), P("tp", None)),
        out_specs=P("dp", None),
        check_vma=False,
    )
```

time: 17.8 us -> 17.3 us (0.972)
  Pallas kernels: 17.7 us -> 17.2 us
    pallas_call x1, Pallas kernels: 16.9 us -> 16.4 us  [step(): pl.pallas_call(block, out_shape=pltpu.VMEM((ROWS, D), bf), in_specs=[anyw...]
where the time goes in v4:
time: 17.3 us
  Pallas kernels  17.2 us (99%)
    pallas_call x1, Pallas kernels, step(): pl.pallas_call(block, out_shape=pltpu.VMEM((ROWS, D), bf), in_specs=[anyw...  16.4 us
    pallas_call x1, Pallas kernels, step(): pl.pallas_call(store, out_shape=jax.ShapeDtypeStruct((ROWS, D), bf), in_s...  0.8 us

profile of v4, /device:TPU:0, one launch (start us, length us, event | category | flops | bytes accessed | tf_op | source)
XLA Modules:
  0.0 17.3 jit_solution(6578361706435184886)
XLA Ops:
  0.0 16.4 %block.1.y_vmem = bf16[128,2048]{1,0:T(8,128)(2,1)S(1)} custom-call(bf16[128,2048]{1,0:T(8,128)(2,1)} %x_hbm.1, bf16[2048,1536]{1,0:T(8,128)(2,1)} %wg_hbm.1, bf16[2048,1536]{1,0:T(8,128)(2,1)} %wu_hbm.1, bf16[1536,2048]{1,0:T(8,128)(2,1)} %wd_hbm.1), custom_call_target="tpu_custom_call" | custom-call | tf_op jit(solution)/shard_map/block/pallas_call | solution.py:216
  16.5 0.8 %store.1 = bf16[128,2048]{1,0:T(8,128)(2,1)} custom-call(bf16[128,2048]{1,0:T(8,128)(2,1)S(1)} %block.1.y_vmem), custom_call_target="tpu_custom_call" | custom-call | tf_op jit(solution)/shard_map/store/pallas_call | solution.py:243

commit v5 on v4

--- a/solution.py
+++ b/solution.py
@@ -13,11 +13,12 @@
 C = 128
 N = D // C
 STEPS = ((0, 1), (2, 3), (4, 5, 6, 7), (8, 9, 10, 11), (12, 13, 14, 15))
-LAG = (1, 2)
-
-GROUPS = (((0, 2), (4, 6), (8,), (10,)), ((5, 7), (9, 11), (12, 13), (14,)))
+SPLIT = (0, 1)
+LAG = ((1, 1, 0, 1, 1), (2, 2, 2, 2, 2))
+
+GROUPS = (((0, 2), (4, 6), (8,), (10,)), ((5, 7), (9, 11), (12,),(13,)))
 DIRECT = (1, 3)
-SHARED = (15,)
+SHARED = (14,15)
 MESH = pl.DeviceIdType.MESH
 scope = jax.named_scope
 OWNER = {k: c for c in range(2) for group in GROUPS[c] for k in group} | {k: 1 for k in DIRECT + SHARED}
@@ -86,9 +87,6 @@
                     part[0, :, :width], part[1, :, :width] = gate, up
                 else:
                     h[:, cols] = (jax.nn.silu(gate) * up).astype(jnp.bfloat16)
-    with scope("barrier"):
-        pl.semaphore_wait(barrier, 3)
-
     def remote(src, dst, recv, to):
         return pltpu.make_async_remote_copy(
             src_ref=src, dst_ref=dst, send_sem=send_sem, recv_sem=recv, device_id={"tp": to}, device_id_type=MESH
@@ -110,10 +108,19 @@
             with scope(f"wait_d{j}"):
                 loaded(wdv.at[:, cols], n)
         with scope(f"down{j}"):
-            value = jnp.dot(h[...], wdv[:, chunks[0] * C : (chunks[-1] + 1) * C], preferred_element_type=f32)
+            cols = slice(chunks[0] * C, (chunks[-1] + 1) * C)
+            if j in SPLIT:
+                width = len(chunks) * C
+                half = [slice(0, F // 2), slice(F // 2, F)]
+                part[me // 4, :, :width] = jnp.dot(h[:, half[0]], wdv[half[0], cols], preferred_element_type=f32)
+                value = jnp.dot(h[:, half[1]], wdv[half[1], cols], preferred_element_type=f32) + part[0, :, :width]
+            else:
+                value = jnp.dot(h[...], wdv[:, cols], preferred_element_type=f32)
             for i, k in enumerate(chunks):
                 own[k] = value[:, i * C : (i + 1) * C]
                 tsend[k] = value[:, i * C : (i + 1) * C].astype(jnp.bfloat16)
+            if j == 0:
+                pl.semaphore_wait(barrier, 3)
             for c in range(2):
 
                 @pl.when(core == c)
@@ -129,31 +136,35 @@
                             sent[c] += 1
 
     def chip_sum(j, c):
-        chunks = [k for k in STEPS[j] if OWNER[k] == c]
+        mine = [k for k in STEPS[j] if OWNER[k] == c]
+        chunks = [k for k in mine if k not in DIRECT]
+        if not chunks:
+            return
+        sent[c] += len(chunks) + 2 * len([k for k in chunks if k in SHARED])
 
         @pl.when(core == c)
         def _():
-            if any(k not in DIRECT for k in chunks):
-                with scope(f"wait_t{j}"):
-                    wait_recv(t_sem.at[j], len(chunks))
+            with scope(f"wait_t{j}"):
+                wait_recv(t_sem.at[j], len(mine))
             for k in chunks:
-                if k in DIRECT:
-                    continue
                 with scope(f"sum{k}"):
                     ssend[k] = (own[k] + trecv[k].astype(f32)).astype(jnp.bfloat16)
                     if k in SHARED:
                         s_copy(k, cross).start()
+                        remote(ssend.at[k], ssend.at[k], b_sem, sib).start()
+                    else:
+                        s_copy(k, opp).start()
+            for k in chunks:
+                if k in SHARED:
                     s_copy(k, opp).start()
-                    if k in SHARED:
-                        remote(ssend.at[k], ssend.at[k], b_sem, sib).start()
-                    sent[c] += 3 if k in SHARED else 1
-
-    for j in range(len(STEPS) + max(LAG)):
+
+    for j in range(len(STEPS) + 3):
         if j < len(STEPS):
             term(j)
         for c in range(2):
-            if 0 <= j - LAG[c] < len(STEPS):
-                chip_sum(j - LAG[c], c)
+            for k in range(len(STEPS)):
+                if k + LAG[c][k] == j:
+                    chip_sum(k, c)
 
     for c in range(2):
 
@@ -198,12 +209,6 @@
                 wait_recv(y_sem, len([k for k in range(N) if OWNER[k] != c and k not in SHARED]))
 
 
-def store(y_vmem, y_hbm, sem):
-    copy = pltpu.make_async_copy(y_vmem, y_hbm, sem)
-    copy.start()
-    copy.wait()
-
-
 def solution(mesh):
     bf = jnp.bfloat16
     dma = pltpu.SemaphoreType.DMA
@@ -213,7 +218,7 @@
     def step(x, w_gate, w_up, w_down):
         hbm = lambda a: pltpu.with_memory_space_constraint(a, pltpu.HBM)
         chunks = lambda n, dtype: pltpu.VMEM((n, ROWS, C), dtype)
-        y = pl.pallas_call(
+        return pl.pallas_call(
             block,
             out_shape=pltpu.VMEM((ROWS, D), bf),
             in_specs=[anywhere] * 4,
@@ -240,14 +245,6 @@
             ),
             name="block",
         )(hbm(x), hbm(w_gate), hbm(w_up), hbm(w_down))
-        return pl.pallas_call(
-            store,
-            out_shape=jax.ShapeDtypeStruct((ROWS, D), bf),
-            in_specs=[vmem],
-            out_specs=anywhere,
-            scratch_shapes=[dma],
-            name="store",
-        )(pltpu.with_memory_space_constraint(y, pltpu.VMEM))
 
     return jax.shard_map(
         step,

time: 17.3 us -> 17 us (0.983)
  Pallas kernels: 17.2 us -> 16.1 us
  local copies, waits for them, and re-layouts: 0 us -> 0.8 us
    pallas_call x1 -> x0, Pallas kernels: 0.8 us -> none  [step(): pl.pallas_call(store, out_shape=jax.ShapeDtypeStruct((ROWS, D), bf), in_s...]
    unnamed x0 -> x1, local copies, waits for them, and re-layouts: none -> 0.8 us
    pallas_call x1, Pallas kernels: 16.4 us -> 16.1 us  [step(): pl.pallas_call(block, out_shape=pltpu.VMEM((ROWS, D), bf), in_specs=[anyw...]
where the time goes in v5:
time: 17 us; the launch traced here: 16.9 us
  Pallas kernels  16.1 us (95%)
  local copies, waits for them, and re-layouts  0.8 us (5%)
    pallas_call x1, Pallas kernels, step(): pl.pallas_call(block, out_shape=pltpu.VMEM((ROWS, D), bf), in_specs=[anyw...  16.1 us
    unnamed x1, local copies, waits for them, and re-layouts  0.8 us

profile of v5, /device:TPU:0, one launch (start us, length us, event | category | flops | bytes accessed | tf_op | source)
XLA Modules:
  0.0 16.9 jit_solution(2987594954044089060)
XLA Ops:
  0.0 16.1 %block.1 = bf16[128,2048]{1,0:T(8,128)(2,1)S(1)} custom-call(bf16[128,2048]{1,0:T(8,128)(2,1)} %x_hbm.1, bf16[2048,1536]{1,0:T(8,128)(2,1)} %wg_hbm.1, bf16[2048,1536]{1,0:T(8,128)(2,1)} %wu_hbm.1, bf16[1536,2048]{1,0:T(8,128)(2,1)} %wd_hbm.1), custom_call_target="tpu_custom_call" | custom-call | tf_op jit(solution)/shard_map/block/pallas_call | solution.py:221
  16.1 0.8 %copy.6 = bf16[128,2048]{1,0:T(8,128)(2,1)} copy(bf16[128,2048]{1,0:T(8,128)(2,1)S(1)} %block.1) | data formatting | bytes 1048576

commit v6 on v5

v6 whole, which is shorter than its diff:
```python
import jax
import jax.numpy as jnp
from jax import lax
from jax.experimental import pallas as pl
from jax.experimental.pallas import tpu as pltpu
from jax.sharding import PartitionSpec as P

ROWS = 128
D = 2048
F = 1536
HIDDEN = ((768, (1024, 1024)), (768, (512, 512, 256, 256, 256, 256)))
DOWN = (256, 256, 512, 1024)
C = 128
N = D // C
STEPS = ((0, 1), (2, 3), (4, 5, 6, 7), (8, 9, 10, 11), (12, 13, 14, 15))
SPLIT = (0, 1)
LAG = ((1, 1, 0, 1, 1), (2, 2, 2, 2, 2))

CUT = {}
GROUPS = (((0, 2, 4, 6), (8, 10)), ((5, 7, 9, 11), (12, 13)))
DIRECT = (1, 3)
SHARED = (14, 15)
MESH = pl.DeviceIdType.MESH
scope = jax.named_scope
OWNER = {k: c for c in range(2) for group in GROUPS[c] for k in group} | {k: 1 for k in DIRECT + SHARED}


def rows(k):
    cut = CUT.get(k % N, ROWS)
    return (0, cut) if k < N else (cut, ROWS - cut)


def stored(k):
    first, n = rows(k)
    return pl.ds((k % N) * ROWS + first, n)


def in_y(k):
    return pl.ds(*rows(k)), pl.ds((k % N) * C, C)


def size(pieces):
    return sum(rows(k)[1] for k in pieces)


def pieces_of(chunks):
    return [k for k in list(chunks) + [N + k for k in chunks if k in CUT]]


def block(x_hbm, wg_hbm, wu_hbm, wd_hbm, out, xv, guv, part, wdv, h, own, tsend, trecv, ssend, srecv, drecv,
          in_sem, t_sem, s_sem, y_sem, send_sem):
    me = lax.axis_index("tp")
    core = lax.rem(me, 2)
    sib = me + 1 - 2 * core
    opp = lax.rem(me + 2, 4)
    cross = 3 - me
    f32 = jnp.float32

    barrier = pltpu.get_barrier_semaphore()
    for other in (sib, opp, cross):
        pl.semaphore_signal(barrier, inc=1, device_id={"tp": other}, device_id_type=MESH)

    loads = []

    def load(ref, *pairs):
        loads.append((ref, pairs))
        return len(loads) - 1

    def start(i):
        for src, dst in loads[i][1]:
            pltpu.make_async_copy(src, dst, in_sem.at[i]).start()

    def loaded(i):
        ref = loads[i][0]
        pltpu.make_async_copy(ref, ref, in_sem.at[i]).wait()

    x_copy = load(xv, (x_hbm, xv))
    hidden, at = [], 0
    for width, depths in HIDDEN:
        cols, top, pieces = pl.ds(at, width), 0, []
        for depth in depths:
            deep = pl.ds(top, depth)
            n = load(
                guv.at[:, deep, cols],
                (wg_hbm.at[deep, cols], guv.at[0, deep, cols]),
                (wu_hbm.at[deep, cols], guv.at[1, deep, cols]),
            )
            pieces.append((n, top, depth))
            top += depth
        hidden.append((at, width, pieces))
        at += width
    down, at = {}, 0
    for width in DOWN:
        cols = pl.ds(at, width)
        down[at // C] = load(wdv.at[:, cols], (wd_hbm.at[:, cols], wdv.at[:, cols]))
        at += width
    for i in range(len(loads)):
        start(i)

    with scope("wait_x"):
        loaded(x_copy)
    for c, (at, width, pieces) in enumerate(hidden):
        cols = slice(at, at + width)
        for n, top, depth in pieces:
            with scope(f"wait_g{c}_{top}"):
                loaded(n)
            with scope(f"hid{c}_{top}"):
                deep = slice(top, top + depth)
                gate = jnp.dot(xv[:, deep], guv[0, deep, cols], preferred_element_type=f32)
                up = jnp.dot(xv[:, deep], guv[1, deep, cols], preferred_element_type=f32)
                if top > 0:
                    gate, up = gate + part[0, :, :width], up + part[1, :, :width]
                if top + depth < D:
                    part[0, :, :width], part[1, :, :width] = gate, up
                else:
                    h[:, cols] = (jax.nn.silu(gate) * up).astype(jnp.bfloat16)
    def remote(src, dst, recv, to):
        return pltpu.make_async_remote_copy(
            src_ref=src, dst_ref=dst, send_sem=send_sem, recv_sem=recv, device_id={"tp": to}, device_id_type=MESH
        )

    def some(n):
        return tsend.at[pl.ds(0, n)], trecv.at[pl.ds(0, n)]

    def wait_recv(sem, n):
        remote(*some(n), sem, sib).wait_recv()

    group_of = {k: g for c in range(2) for g, group in enumerate(GROUPS[c]) for k in group}
    shared_sem = s_sem.at[max(len(groups) for groups in GROUPS)]
    t_slot = lambda j, c: t_sem.at[j - min(i for i in range(len(STEPS)) if summed(i, c))]
    s_copy = lambda k, to: remote(
        ssend.at[stored(k)], srecv.at[stored(k)], shared_sem if k in SHARED else s_sem.at[group_of[k]], to
    )
    d_sem = t_sem.at[len(STEPS) - 2]
    sent = {0: 0, 1: 0}

    def summed(j, c):
        return [k for k in pieces_of(STEPS[j]) if OWNER[k] == c and k not in DIRECT]

    def term(j):
        chunks = STEPS[j]
        if chunks[0] in down:
            with scope(f"wait_d{j}"):
                loaded(down[chunks[0]])
        with scope(f"down{j}"):
            cols = slice(chunks[0] * C, (chunks[-1] + 1) * C)
            if j in SPLIT:
                width = len(chunks) * C
                half = [slice(0, F // 2), slice(F // 2, F)]
                part[me // 4, :, :width] = jnp.dot(h[:, half[0]], wdv[half[0], cols], preferred_element_type=f32)
                value = jnp.dot(h[:, half[1]], wdv[half[1], cols], preferred_element_type=f32) + part[0, :, :width]
            else:
                value = jnp.dot(h[...], wdv[:, cols], preferred_element_type=f32)
            for i, k in enumerate(chunks):
                at = slice(k * ROWS, (k + 1) * ROWS)
                own[at] = value[:, i * C : (i + 1) * C]
                tsend[at] = value[:, i * C : (i + 1) * C].astype(jnp.bfloat16)
            if j == 0:
                pl.semaphore_wait(barrier, 3)
            pieces = pieces_of(chunks)
            for c in range(2):

                @pl.when(core == c)
                def _(c=c):
                    for k in pieces:
                        if k in DIRECT:
                            place = drecv.at[c, stored(k)]
                            remote(tsend.at[stored(k)], place, d_sem, opp if c == OWNER[k] else cross).start()
                            sent[c] += size([k])
                    for k in pieces:
                        if OWNER[k] != c:
                            sem = d_sem if k in DIRECT else t_slot(j, OWNER[k])
                            remote(tsend.at[stored(k)], trecv.at[stored(k)], sem, sib).start()
                            sent[c] += size([k])

    def chip_sum(j, c):
        pieces = summed(j, c)
        if not pieces:
            return
        sent[c] += size(pieces) + 2 * size([k for k in pieces if k in SHARED])

        @pl.when(core == c)
        def _():
            with scope(f"wait_t{j}"):
                wait_recv(t_slot(j, c), size(pieces))
            for k in pieces:
                with scope(f"sum{k}"):
                    at = stored(k)
                    ssend[at] = (own[at] + trecv[at].astype(f32)).astype(jnp.bfloat16)
                    if k in SHARED:
                        s_copy(k, cross).start()
                        remote(ssend.at[at], ssend.at[at], shared_sem, sib).start()
                    else:
                        s_copy(k, opp).start()
            for k in pieces:
                if k in SHARED:
                    s_copy(k, opp).start()

    for j in range(len(STEPS) + 3):
        if j < len(STEPS):
            term(j)
        for c in range(2):
            for k in range(len(STEPS)):
                if k + LAG[c][k] == j:
                    chip_sum(k, c)

    for c in range(2):

        @pl.when(core == c)
        def _(c=c):
            def finish(k, here, there):
                with scope(f"fin{k}"):
                    out[in_y(k)] = (here + there).astype(jnp.bfloat16)
                    if k not in SHARED:
                        place = out.at[in_y(k)]
                        remote(place, place, y_sem, sib).start()
                        sent[c] += size([k])

            if c == 1 and DIRECT:
                with scope("wait_direct"):
                    wait_recv(d_sem, 3 * size(DIRECT))
                for k in DIRECT:
                    at = stored(k)
                    here = tsend[at].astype(f32) + trecv[at].astype(f32)
                    finish(k, here, drecv[1, at].astype(f32) + drecv[0, at].astype(f32))
            for g, group in enumerate(GROUPS[c]):
                with scope(f"wait_s{group[0]}"):
                    wait_recv(s_sem.at[g], size(group))
                for k in group:
                    finish(k, ssend[stored(k)].astype(f32), srecv[stored(k)].astype(f32))
            if SHARED:
                with scope("wait_shared"):
                    wait_recv(shared_sem, size(SHARED) * (2 - c))
            for k in SHARED:
                finish(k, ssend[stored(k)].astype(f32), srecv[stored(k)].astype(f32))
            with scope("drain_send"):
                total = sent[c]
                while total:
                    n = min(total, N * ROWS)
                    remote(*some(n), y_sem, sib).wait_send()
                    total -= n
            with scope("drain_y"):
                wait_recv(y_sem, size([k for k in OWNER if OWNER[k] != c and k not in SHARED]))


def solution(mesh):
    bf = jnp.bfloat16
    dma = pltpu.SemaphoreType.DMA
    anywhere = pl.BlockSpec(memory_space=pl.ANY)
    vmem = pl.BlockSpec(memory_space=pltpu.VMEM)

    def step(x, w_gate, w_up, w_down):
        hbm = lambda a: pltpu.with_memory_space_constraint(a, pltpu.HBM)
        chunks = lambda dtype: pltpu.VMEM((N * ROWS, C), dtype)
        return pl.pallas_call(
            block,
            out_shape=pltpu.VMEM((ROWS, D), bf),
            in_specs=[anywhere] * 4,
            out_specs=vmem,
            scratch_shapes=[
                pltpu.VMEM((ROWS, D), bf),
                pltpu.VMEM((2, D, F), bf),
                pltpu.VMEM((2, ROWS, max(width for width, _ in HIDDEN)), jnp.float32),
                pltpu.VMEM((F, D), bf),
                pltpu.VMEM((ROWS, F), bf),
                chunks(jnp.float32),
                chunks(bf),
                chunks(bf),
                chunks(bf),
                chunks(bf),
                pltpu.VMEM((2, N * ROWS, C), bf),
                dma((1 + sum(len(depths) for _, depths in HIDDEN) + len(DOWN),)),
                dma((len(STEPS) - 1,)),
                dma((1 + max(len(groups) for groups in GROUPS),)),
                *[dma] * 2,
            ],
            compiler_params=pltpu.CompilerParams(
                collective_id=0, has_side_effects=True, vmem_limit_bytes=50 * 2**20
            ),
            name="block",
        )(hbm(x), hbm(w_gate), hbm(w_up), hbm(w_down))

    return jax.shard_map(
        step,
        mesh=mesh,
        in_specs=(P("dp", None), P(None, "tp"), P(None, "tp"), P("tp", None)),
        out_specs=P("dp", None),
        check_vma=False,
    )
```

time: 17 us -> 16.9 us (level)
  no operation moved by 1% of the time
where the time goes in v6:
time: 16.9 us; the launch traced here: 16.8 us
  Pallas kernels  16 us (95%)
  local copies, waits for them, and re-layouts  0.8 us (5%)
    pallas_call x1, Pallas kernels, step(): pl.pallas_call(block, out_shape=pltpu.VMEM((ROWS, D), bf), in_specs=[anyw...  16 us
    unnamed x1, local copies, waits for them, and re-layouts  0.8 us

profile of v6, /device:TPU:0, one launch (start us, length us, event | category | flops | bytes accessed | tf_op | source)
XLA Modules:
  0.0 16.8 jit_solution(4337376417856845566)
XLA Ops:
  0.0 16.0 %block.1 = bf16[128,2048]{1,0:T(8,128)(2,1)S(1)} custom-call(bf16[128,2048]{1,0:T(8,128)(2,1)} %x_hbm.1, bf16[2048,1536]{1,0:T(8,128)(2,1)} %wg_hbm.1, bf16[2048,1536]{1,0:T(8,128)(2,1)} %wu_hbm.1, bf16[1536,2048]{1,0:T(8,128)(2,1)} %wd_hbm.1), custom_call_target="tpu_custom_call" | custom-call | tf_op jit(solution)/shard_map/block/pallas_call | solution.py:255
  16.0 0.8 %copy.6 = bf16[128,2048]{1,0:T(8,128)(2,1)} copy(bf16[128,2048]{1,0:T(8,128)(2,1)S(1)} %block.1) | data formatting | bytes 1048576

commit v7 on v6

--- a/solution.py
+++ b/solution.py
@@ -10,9 +10,10 @@
 F = 1536
 HIDDEN = ((768, (1024, 1024)), (768, (512, 512, 256, 256, 256, 256)))
 DOWN = (256, 256, 512, 1024)
+STEPS = ((0, 1), (2, 3), (4, 5, 6, 7), (8, 9, 10, 11), (12, 13, 14, 15))
+LENT = 4
 C = 128
 N = D // C
-STEPS = ((0, 1), (2, 3), (4, 5, 6, 7), (8, 9, 10, 11), (12, 13, 14, 15))
 SPLIT = (0, 1)
 LAG = ((1, 1, 0, 1, 1), (2, 2, 2, 2, 2))
 
@@ -48,17 +49,21 @@
 
 
 def block(x_hbm, wg_hbm, wu_hbm, wd_hbm, out, xv, guv, part, wdv, h, own, tsend, trecv, ssend, srecv, drecv,
-          in_sem, t_sem, s_sem, y_sem, send_sem):
+          in_sem, s_sem):
     me = lax.axis_index("tp")
     core = lax.rem(me, 2)
     sib = me + 1 - 2 * core
     opp = lax.rem(me + 2, 4)
     cross = 3 - me
     f32 = jnp.float32
+    n_in = 1 + sum(len(depths) for _, depths in HIDDEN) + len(DOWN)
+    t_sem, y_sem, send_sem = in_sem, in_sem.at[n_in], in_sem.at[LENT]
 
     barrier = pltpu.get_barrier_semaphore()
-    for other in (sib, opp, cross):
-        pl.semaphore_signal(barrier, inc=1, device_id={"tp": other}, device_id_type=MESH)
+
+    def announce():
+        for other in (sib, opp, cross):
+            pl.semaphore_signal(barrier, inc=1, device_id={"tp": other}, device_id_type=MESH)
 
     loads = []
 
@@ -104,6 +109,8 @@
         for n, top, depth in pieces:
             with scope(f"wait_g{c}_{top}"):
                 loaded(n)
+            if n == LENT - 1:
+                announce()
             with scope(f"hid{c}_{top}"):
                 deep = slice(top, top + depth)
                 gate = jnp.dot(xv[:, deep], guv[0, deep, cols], preferred_element_type=f32)
@@ -269,10 +276,8 @@
                 chunks(bf),
                 chunks(bf),
                 pltpu.VMEM((2, N * ROWS, C), bf),
-                dma((1 + sum(len(depths) for _, depths in HIDDEN) + len(DOWN),)),
-                dma((len(STEPS) - 1,)),
+                dma((2 + sum(len(depths) for _, depths in HIDDEN) + len(DOWN),)),
                 dma((1 + max(len(groups) for groups in GROUPS),)),
-                *[dma] * 2,
             ],
             compiler_params=pltpu.CompilerParams(
                 collective_id=0, has_side_effects=True, vmem_limit_bytes=50 * 2**20

time: 16.9 us -> 16.8 us (level)
  no operation moved by 1% of the time
where the time goes in v7:
time: 16.8 us; the launch traced here: 16.7 us
  Pallas kernels  15.9 us (95%)
  local copies, waits for them, and re-layouts  0.8 us (5%)
    pallas_call x1, Pallas kernels, step(): pl.pallas_call(block, out_shape=pltpu.VMEM((ROWS, D), bf), in_specs=[anyw...  15.9 us
    unnamed x1, local copies, waits for them, and re-layouts  0.8 us

profile of v7, /device:TPU:0, one launch (start us, length us, event | category | flops | bytes accessed | tf_op | source)
XLA Modules:
  0.0 16.7 jit_solution(2666957634728557279)
XLA Ops:
  0.0 15.9 %block.1 = bf16[128,2048]{1,0:T(8,128)(2,1)S(1)} custom-call(bf16[128,2048]{1,0:T(8,128)(2,1)} %x_hbm.1, bf16[2048,1536]{1,0:T(8,128)(2,1)} %wg_hbm.1, bf16[2048,1536]{1,0:T(8,128)(2,1)} %wu_hbm.1, bf16[1536,2048]{1,0:T(8,128)(2,1)} %wd_hbm.1), custom_call_target="tpu_custom_call" | custom-call | tf_op jit(solution)/shard_map/block/pallas_call | solution.py:262
  16.0 0.8 %copy.6 = bf16[128,2048]{1,0:T(8,128)(2,1)} copy(bf16[128,2048]{1,0:T(8,128)(2,1)S(1)} %block.1) | data formatting | bytes 1048576

commit v8 on v7

--- a/solution.py
+++ b/solution.py
@@ -8,7 +8,7 @@
 ROWS = 128
 D = 2048
 F = 1536
-HIDDEN = ((768, (1024, 1024)), (768, (512, 512, 256, 256, 256, 256)))
+HIDDEN = ((768, (1024, 1024)), (768, (768, 512, 256, 256, 256)))
 DOWN = (256, 256, 512, 1024)
 STEPS = ((0, 1), (2, 3), (4, 5, 6, 7), (8, 9, 10, 11), (12, 13, 14, 15))
 LENT = 4
@@ -56,8 +56,7 @@
     opp = lax.rem(me + 2, 4)
     cross = 3 - me
     f32 = jnp.float32
-    n_in = 1 + sum(len(depths) for _, depths in HIDDEN) + len(DOWN)
-    t_sem, y_sem, send_sem = in_sem, in_sem.at[n_in], in_sem.at[LENT]
+    t_sem, send_sem, y_sem = in_sem, in_sem.at[LENT], in_sem.at[LENT + 1]
 
     barrier = pltpu.get_barrier_semaphore()
 
@@ -160,7 +159,8 @@
                 value = jnp.dot(h[...], wdv[:, cols], preferred_element_type=f32)
             for i, k in enumerate(chunks):
                 at = slice(k * ROWS, (k + 1) * ROWS)
-                own[at] = value[:, i * C : (i + 1) * C]
+                if k not in DIRECT:
+                    own[at] = value[:, i * C : (i + 1) * C]
                 tsend[at] = value[:, i * C : (i + 1) * C].astype(jnp.bfloat16)
             if j == 0:
                 pl.semaphore_wait(barrier, 3)
@@ -276,7 +276,7 @@
                 chunks(bf),
                 chunks(bf),
                 pltpu.VMEM((2, N * ROWS, C), bf),
-                dma((2 + sum(len(depths) for _, depths in HIDDEN) + len(DOWN),)),
+                dma((1 + sum(len(depths) for _, depths in HIDDEN) + len(DOWN),)),
                 dma((1 + max(len(groups) for groups in GROUPS),)),
             ],
             compiler_params=pltpu.CompilerParams(

time: 16.8 us -> 16.8 us (level)
  no operation moved by 1% of the time
where the time goes in v8:
time: 16.8 us; the launch traced here: 16.7 us
  Pallas kernels  15.9 us (95%)
  local copies, waits for them, and re-layouts  0.8 us (5%)
    pallas_call x1, Pallas kernels, step(): pl.pallas_call(block, out_shape=pltpu.VMEM((ROWS, D), bf), in_specs=[anyw...  15.9 us
    unnamed x1, local copies, waits for them, and re-layouts  0.8 us

profile of v8, /device:TPU:0, one launch (start us, length us, event | category | flops | bytes accessed | tf_op | source)
XLA Modules:
  0.0 16.7 jit_solution(4907044330936530285)
XLA Ops:
  0.0 15.9 %block.1 = bf16[128,2048]{1,0:T(8,128)(2,1)S(1)} custom-call(bf16[128,2048]{1,0:T(8,128)(2,1)} %x_hbm.1, bf16[2048,1536]{1,0:T(8,128)(2,1)} %wg_hbm.1, bf16[2048,1536]{1,0:T(8,128)(2,1)} %wu_hbm.1, bf16[1536,2048]{1,0:T(8,128)(2,1)} %wd_hbm.1), custom_call_target="tpu_custom_call" | custom-call | tf_op jit(solution)/shard_map/block/pallas_call | solution.py:262
  15.9 0.8 %copy.6 = bf16[128,2048]{1,0:T(8,128)(2,1)} copy(bf16[128,2048]{1,0:T(8,128)(2,1)S(1)} %block.1) | data formatting | bytes 1048576

commit v9 on v8

--- a/solution.py
+++ b/solution.py
@@ -18,9 +18,12 @@
 LAG = ((1, 1, 0, 1, 1), (2, 2, 2, 2, 2))
 
 CUT = {}
-GROUPS = (((0, 2, 4, 6), (8, 10)), ((5, 7, 9, 11), (12, 13)))
+GROUPS = (((0, 2, 6), (8, 10), (4,)), ((5, 7, 9, 11), (12, 13)))
 DIRECT = (1, 3)
 SHARED = (14, 15)
+DETOUR = 4
+RELAY_STEP = 3
+SOURCE, RELAY, TARGET, GIVER = ({"dp": d, "tp": t} for d, t in ((0, 2), (1, 3), (0, 1), (0, 0)))
 MESH = pl.DeviceIdType.MESH
 scope = jax.named_scope
 OWNER = {k: c for c in range(2) for group in GROUPS[c] for k in group} | {k: 1 for k in DIRECT + SHARED}
@@ -49,8 +52,11 @@
 
 
 def block(x_hbm, wg_hbm, wu_hbm, wd_hbm, out, xv, guv, part, wdv, h, own, tsend, trecv, ssend, srecv, drecv,
-          in_sem, s_sem):
+          relayed, in_sem, s_sem, relay_sem):
     me = lax.axis_index("tp")
+    dp = lax.axis_index("dp")
+    at_place = lambda place: jnp.logical_and(dp == place["dp"], me == place["tp"])
+    not_at = lambda place: jnp.logical_or(dp != place["dp"], me != place["tp"])
     core = lax.rem(me, 2)
     sib = me + 1 - 2 * core
     opp = lax.rem(me + 2, 4)
@@ -63,6 +69,11 @@
     def announce():
         for other in (sib, opp, cross):
             pl.semaphore_signal(barrier, inc=1, device_id={"tp": other}, device_id_type=MESH)
+        for receiver, sender in ((RELAY, SOURCE), (TARGET, RELAY)):
+
+            @pl.when(at_place(receiver))
+            def _(sender=sender):
+                pl.semaphore_signal(barrier, inc=1, device_id=sender, device_id_type=MESH)
 
     loads = []
 
@@ -122,7 +133,12 @@
                     h[:, cols] = (jax.nn.silu(gate) * up).astype(jnp.bfloat16)
     def remote(src, dst, recv, to):
         return pltpu.make_async_remote_copy(
-            src_ref=src, dst_ref=dst, send_sem=send_sem, recv_sem=recv, device_id={"tp": to}, device_id_type=MESH
+            src_ref=src,
+            dst_ref=dst,
+            send_sem=send_sem,
+            recv_sem=recv,
+            device_id=to if isinstance(to, dict) else {"tp": to},
+            device_id_type=MESH,
         )
 
     def some(n):
@@ -163,7 +179,8 @@
                     own[at] = value[:, i * C : (i + 1) * C]
                 tsend[at] = value[:, i * C : (i + 1) * C].astype(jnp.bfloat16)
             if j == 0:
-                pl.semaphore_wait(barrier, 3)
+                more = jnp.logical_or(at_place(SOURCE), at_place(RELAY)).astype(jnp.int32)
+                pl.semaphore_wait(barrier, 3 + more)
             pieces = pieces_of(chunks)
             for c in range(2):
 
@@ -188,6 +205,14 @@
 
         @pl.when(core == c)
         def _():
+            if c == 1 and j == RELAY_STEP:
+
+                @pl.when(at_place(RELAY))
+                def _():
+                    with scope("relay"):
+                        wait_recv(relay_sem, size([DETOUR]))
+                        remote(relayed, srecv.at[stored(DETOUR)], s_sem.at[group_of[DETOUR]], TARGET).start()
+
             with scope(f"wait_t{j}"):
                 wait_recv(t_slot(j, c), size(pieces))
             for k in pieces:
@@ -197,6 +222,20 @@
                     if k in SHARED:
                         s_copy(k, cross).start()
                         remote(ssend.at[at], ssend.at[at], shared_sem, sib).start()
+                    elif k == DETOUR:
+
+                        @pl.when(at_place(SOURCE))
+                        def _(at=at):
+                            remote(ssend.at[at], relayed, relay_sem, RELAY).start()
+
+                        @pl.when(not_at(SOURCE))
+                        def _(k=k):
+                            s_copy(k, opp).start()
+
+                        @pl.when(at_place(GIVER))
+                        def _(at=at):
+                            remote(ssend.at[at], ssend.at[at], relay_sem, sib).start()
+
                     else:
                         s_copy(k, opp).start()
             for k in pieces:
@@ -230,24 +269,45 @@
                     at = stored(k)
                     here = tsend[at].astype(f32) + trecv[at].astype(f32)
                     finish(k, here, drecv[1, at].astype(f32) + drecv[0, at].astype(f32))
-            for g, group in enumerate(GROUPS[c]):
+            def finish_group(g, group):
                 with scope(f"wait_s{group[0]}"):
                     wait_recv(s_sem.at[g], size(group))
                 for k in group:
                     finish(k, ssend[stored(k)].astype(f32), srecv[stored(k)].astype(f32))
+
+            for g, group in enumerate(GROUPS[c]):
+                if DETOUR in group:
+                    pl.when(not_at(GIVER))(lambda g=g, group=group: finish_group(g, group))
+                else:
+                    finish_group(g, group)
+                if c == 1 and g == 0:
+
+                    @pl.when(at_place(TARGET))
+                    def _():
+                        wait_recv(relay_sem, size([DETOUR]))
+                        finish_group(group_of[DETOUR], [DETOUR])
+                        sent[c] -= size([DETOUR])
+
             if SHARED:
                 with scope("wait_shared"):
                     wait_recv(shared_sem, size(SHARED) * (2 - c))
             for k in SHARED:
                 finish(k, ssend[stored(k)].astype(f32), srecv[stored(k)].astype(f32))
-            with scope("drain_send"):
-                total = sent[c]
-                while total:
-                    n = min(total, N * ROWS)
-                    remote(*some(n), y_sem, sib).wait_send()
-                    total -= n
-            with scope("drain_y"):
-                wait_recv(y_sem, size([k for k in OWNER if OWNER[k] != c and k not in SHARED]))
+            with scope("drain"):
+                come = size([k for k in OWNER if OWNER[k] != c and k not in SHARED])
+                more = size([DETOUR])
+                cases = [(at_place(GIVER), 0, more)] if c == 0 else [(at_place(TARGET), more, -more), (at_place(RELAY), more, 0)]
+                cases.append((not_at(GIVER) if c == 0 else jnp.logical_and(not_at(TARGET), not_at(RELAY)), 0, 0))
+                for place, extra_sent, extra_come in cases:
+
+                    @pl.when(place)
+                    def _(extra_sent=extra_sent, extra_come=extra_come):
+                        total = sent[c] + extra_sent
+                        while total:
+                            n = min(total, N * ROWS)
+                            remote(*some(n), y_sem, sib).wait_send()
+                            total -= n
+                        wait_recv(y_sem, come + extra_come)
 
 
 def solution(mesh):
@@ -276,8 +336,10 @@
                 chunks(bf),
                 chunks(bf),
                 pltpu.VMEM((2, N * ROWS, C), bf),
+                pltpu.VMEM((ROWS, C), bf),
                 dma((1 + sum(len(depths) for _, depths in HIDDEN) + len(DOWN),)),
                 dma((1 + max(len(groups) for groups in GROUPS),)),
+                dma,
             ],
             compiler_params=pltpu.CompilerParams(
                 collective_id=0, has_side_effects=True, vmem_limit_bytes=50 * 2**20

time: 16.8 us -> 16.6 us (0.988)
  Pallas kernels: 15.9 us -> 15.7 us
    pallas_call x1, Pallas kernels: 15.9 us -> 15.7 us  [step(): pl.pallas_call(block, out_shape=pltpu.VMEM((ROWS, D), bf), in_specs=[anyw...]
where the time goes in v9:
time: 16.6 us; the launch traced here: 16.5 us
  Pallas kernels  15.7 us (95%)
  local copies, waits for them, and re-layouts  0.8 us (5%)
    pallas_call x1, Pallas kernels, step(): pl.pallas_call(block, out_shape=pltpu.VMEM((ROWS, D), bf), in_specs=[anyw...  15.7 us
    unnamed x1, local copies, waits for them, and re-layouts  0.8 us

profile of v9, /device:TPU:0, one launch (start us, length us, event | category | flops | bytes accessed | tf_op | source)
XLA Modules:
  0.0 16.5 jit_solution(5509985705753000576)
XLA Ops:
  0.0 15.7 %block.1 = bf16[128,2048]{1,0:T(8,128)(2,1)S(1)} custom-call(bf16[128,2048]{1,0:T(8,128)(2,1)} %x_hbm.1, bf16[2048,1536]{1,0:T(8,128)(2,1)} %wg_hbm.1, bf16[2048,1536]{1,0:T(8,128)(2,1)} %wu_hbm.1, bf16[1536,2048]{1,0:T(8,128)(2,1)} %wd_hbm.1), custom_call_target="tpu_custom_call" | custom-call | tf_op jit(solution)/shard_map/block/pallas_call | solution.py:322
  15.7 0.8 %copy.6 = bf16[128,2048]{1,0:T(8,128)(2,1)} copy(bf16[128,2048]{1,0:T(8,128)(2,1)S(1)} %block.1) | data formatting | bytes 1048576

commit v10 on v9

--- a/solution.py
+++ b/solution.py
@@ -17,11 +17,11 @@
 SPLIT = (0, 1)
 LAG = ((1, 1, 0, 1, 1), (2, 2, 2, 2, 2))
 
-CUT = {}
-GROUPS = (((0, 2, 6), (8, 10), (4,)), ((5, 7, 9, 11), (12, 13)))
+CUT = {4: 48}
+GROUPS = (((0, 2, 6), (8, 10), (4, 20)), ((5, 7, 9, 11), (12, 13)))
 DIRECT = (1, 3)
 SHARED = (14, 15)
-DETOUR = 4
+DETOUR = (4, 20)
 RELAY_STEP = 3
 SOURCE, RELAY, TARGET, GIVER = ({"dp": d, "tp": t} for d, t in ((0, 2), (1, 3), (0, 1), (0, 0)))
 MESH = pl.DeviceIdType.MESH
@@ -210,8 +210,10 @@
                 @pl.when(at_place(RELAY))
                 def _():
                     with scope("relay"):
-                        wait_recv(relay_sem, size([DETOUR]))
-                        remote(relayed, srecv.at[stored(DETOUR)], s_sem.at[group_of[DETOUR]], TARGET).start()
+                        for i, k in enumerate(DETOUR):
+                            wait_recv(relay_sem.at[i], size([k]))
+                            place = srecv.at[stored(k)]
+                            remote(relayed.at[pl.ds(*rows(k))], place, s_sem.at[group_of[k]], TARGET).start()
 
             with scope(f"wait_t{j}"):
                 wait_recv(t_slot(j, c), size(pieces))
@@ -222,11 +224,12 @@
                     if k in SHARED:
                         s_copy(k, cross).start()
                         remote(ssend.at[at], ssend.at[at], shared_sem, sib).start()
-                    elif k == DETOUR:
+                    elif k in DETOUR:
 
                         @pl.when(at_place(SOURCE))
-                        def _(at=at):
-                            remote(ssend.at[at], relayed, relay_sem, RELAY).start()
+                        def _(k=k, at=at):
+                            place = relayed.at[pl.ds(*rows(k))]
+                            remote(ssend.at[at], place, relay_sem.at[DETOUR.index(k)], RELAY).start()
 
                         @pl.when(not_at(SOURCE))
                         def _(k=k):
@@ -234,7 +237,7 @@
 
                         @pl.when(at_place(GIVER))
                         def _(at=at):
-                            remote(ssend.at[at], ssend.at[at], relay_sem, sib).start()
+                            remote(ssend.at[at], ssend.at[at], relay_sem.at[0], sib).start()
 
                     else:
                         s_copy(k, opp).start()
@@ -276,7 +279,7 @@
                     finish(k, ssend[stored(k)].astype(f32), srecv[stored(k)].astype(f32))
 
             for g, group in enumerate(GROUPS[c]):
-                if DETOUR in group:
+                if DETOUR == group:
                     pl.when(not_at(GIVER))(lambda g=g, group=group: finish_group(g, group))
                 else:
                     finish_group(g, group)
@@ -284,9 +287,9 @@
 
                     @pl.when(at_place(TARGET))
                     def _():
-                        wait_recv(relay_sem, size([DETOUR]))
-                        finish_group(group_of[DETOUR], [DETOUR])
-                        sent[c] -= size([DETOUR])
+                        wait_recv(relay_sem.at[0], size(DETOUR))
+                        finish_group(group_of[DETOUR[0]], DETOUR)
+                        sent[c] -= size(DETOUR)
 
             if SHARED:
                 with scope("wait_shared"):
@@ -295,7 +298,7 @@
                 finish(k, ssend[stored(k)].astype(f32), srecv[stored(k)].astype(f32))
             with scope("drain"):
                 come = size([k for k in OWNER if OWNER[k] != c and k not in SHARED])
-                more = size([DETOUR])
+                more = size(DETOUR)
                 cases = [(at_place(GIVER), 0, more)] if c == 0 else [(at_place(TARGET), more, -more), (at_place(RELAY), more, 0)]
                 cases.append((not_at(GIVER) if c == 0 else jnp.logical_and(not_at(TARGET), not_at(RELAY)), 0, 0))
                 for place, extra_sent, extra_come in cases:
@@ -339,7 +342,7 @@
                 pltpu.VMEM((ROWS, C), bf),
                 dma((1 + sum(len(depths) for _, depths in HIDDEN) + len(DOWN),)),
                 dma((1 + max(len(groups) for groups in GROUPS),)),
-                dma,
+                dma((len(DETOUR),)),
             ],
             compiler_params=pltpu.CompilerParams(
                 collective_id=0, has_side_effects=True, vmem_limit_bytes=50 * 2**20

time: 16.6 us -> 16.5 us (level)
  no operation moved by 1% of the time
where the time goes in v10:
time: 16.5 us; the launch traced here: 16.4 us
  Pallas kernels  15.6 us (95%)
  local copies, waits for them, and re-layouts  0.8 us (5%)
    pallas_call x1, Pallas kernels, step(): pl.pallas_call(block, out_shape=pltpu.VMEM((ROWS, D), bf), in_specs=[anyw...  15.6 us
    unnamed x1, local copies, waits for them, and re-layouts  0.8 us

profile of v10, /device:TPU:0, one launch (start us, length us, event | category | flops | bytes accessed | tf_op | source)
XLA Modules:
  0.0 16.4 jit_solution(3996172566651714241)
XLA Ops:
  0.0 15.6 %block.1 = bf16[128,2048]{1,0:T(8,128)(2,1)S(1)} custom-call(bf16[128,2048]{1,0:T(8,128)(2,1)} %x_hbm.1, bf16[2048,1536]{1,0:T(8,128)(2,1)} %wg_hbm.1, bf16[2048,1536]{1,0:T(8,128)(2,1)} %wu_hbm.1, bf16[1536,2048]{1,0:T(8,128)(2,1)} %wd_hbm.1), custom_call_target="tpu_custom_call" | custom-call | tf_op jit(solution)/shard_map/block/pallas_call | solution.py:325
  15.6 0.8 %copy.6 = bf16[128,2048]{1,0:T(8,128)(2,1)} copy(bf16[128,2048]{1,0:T(8,128)(2,1)S(1)} %block.1) | data formatting | bytes 1048576

commit v11 on v10

--- a/solution.py
+++ b/solution.py
@@ -148,6 +148,7 @@
         remote(*some(n), sem, sib).wait_recv()
 
     group_of = {k: g for c in range(2) for g, group in enumerate(GROUPS[c]) for k in group}
+    relay_sems = (s_sem.at[group_of[DETOUR[0]]], relay_sem)
     shared_sem = s_sem.at[max(len(groups) for groups in GROUPS)]
     t_slot = lambda j, c: t_sem.at[j - min(i for i in range(len(STEPS)) if summed(i, c))]
     s_copy = lambda k, to: remote(
@@ -211,7 +212,7 @@
                 def _():
                     with scope("relay"):
                         for i, k in enumerate(DETOUR):
-                            wait_recv(relay_sem.at[i], size([k]))
+                            wait_recv(relay_sems[i], size([k]))
                             place = srecv.at[stored(k)]
                             remote(relayed.at[pl.ds(*rows(k))], place, s_sem.at[group_of[k]], TARGET).start()
 
@@ -229,7 +230,7 @@
                         @pl.when(at_place(SOURCE))
                         def _(k=k, at=at):
                             place = relayed.at[pl.ds(*rows(k))]
-                            remote(ssend.at[at], place, relay_sem.at[DETOUR.index(k)], RELAY).start()
+                            remote(ssend.at[at], place, relay_sems[DETOUR.index(k)], RELAY).start()
 
                         @pl.when(not_at(SOURCE))
                         def _(k=k):
@@ -237,7 +238,7 @@
 
                         @pl.when(at_place(GIVER))
                         def _(at=at):
-                            remote(ssend.at[at], ssend.at[at], relay_sem.at[0], sib).start()
+                            remote(ssend.at[at], ssend.at[at], relay_sems[0], sib).start()
 
                     else:
                         s_copy(k, opp).start()
@@ -287,8 +288,9 @@
 
                     @pl.when(at_place(TARGET))
                     def _():
-                        wait_recv(relay_sem.at[0], size(DETOUR))
-                        finish_group(group_of[DETOUR[0]], DETOUR)
+                        wait_recv(relay_sems[0], 2 * size(DETOUR))
+                        for k in DETOUR:
+                            finish(k, ssend[stored(k)].astype(f32), srecv[stored(k)].astype(f32))
                         sent[c] -= size(DETOUR)
 
             if SHARED:
@@ -342,7 +344,7 @@
                 pltpu.VMEM((ROWS, C), bf),
                 dma((1 + sum(len(depths) for _, depths in HIDDEN) + len(DOWN),)),
                 dma((1 + max(len(groups) for groups in GROUPS),)),
-                dma((len(DETOUR),)),
+                dma,
             ],
             compiler_params=pltpu.CompilerParams(
                 collective_id=0, has_side_effects=True, vmem_limit_bytes=50 * 2**20

time: 16.5 us -> 16.5 us (level)
  no operation moved by 1% of the time
where the time goes in v11:
time: 16.5 us; the launch traced here: 16.4 us
  Pallas kernels  15.6 us (95%)
  local copies, waits for them, and re-layouts  0.8 us (5%)
    pallas_call x1, Pallas kernels, step(): pl.pallas_call(block, out_shape=pltpu.VMEM((ROWS, D), bf), in_specs=[anyw...  15.6 us
    unnamed x1, local copies, waits for them, and re-layouts  0.8 us

profile of v11, /device:TPU:0, one launch (start us, length us, event | category | flops | bytes accessed | tf_op | source)
XLA Modules:
  0.0 16.4 jit_solution(11480479413977010782)
XLA Ops:
  0.0 15.6 %block.1 = bf16[128,2048]{1,0:T(8,128)(2,1)S(1)} custom-call(bf16[128,2048]{1,0:T(8,128)(2,1)} %x_hbm.1, bf16[2048,1536]{1,0:T(8,128)(2,1)} %wg_hbm.1, bf16[2048,1536]{1,0:T(8,128)(2,1)} %wu_hbm.1, bf16[1536,2048]{1,0:T(8,128)(2,1)} %wd_hbm.1), custom_call_target="tpu_custom_call" | custom-call | tf_op jit(solution)/shard_map/block/pallas_call | solution.py:327
  15.6 0.8 %copy.6 = bf16[128,2048]{1,0:T(8,128)(2,1)} copy(bf16[128,2048]{1,0:T(8,128)(2,1)S(1)} %block.1) | data formatting | bytes 1048576
